TPU v7x, 32 devices: a whole 2x2x4 slice. The times are simulated.
32 devices in a mesh: seq: 4 (over y, x), batch: 8 (over z, core).
Axes of the slice: x: 2, y: 2, z: 4, core: 2. Of those that a mesh axis runs over, the one named last changes fastest.
Arguments:
- attn_out: bfloat16 [16384, 2560], P(('seq', 'batch')), may hold values from -200 to 200
- out_grad: bfloat16 [16384, 2560], P(('seq', 'batch')), may hold values from -6 to 6
- master: float32 [2560, 2560], P(('seq', 'batch')), may hold values from -0.125 to 0.125
- moment_one: float32 [2560, 2560], P(('seq', 'batch')), may hold values from -4 to 4
- moment_two: float32 [2560, 2560], P(('seq', 'batch')), may hold values from 0.002 to 0.05
Outputs:
- input_grad: bfloat16 [16384, 2560], P(('seq', 'batch'))
- new_master: float32 [2560, 2560], P(('seq', 'batch'))
- new_moment_one: float32 [2560, 2560], P(('seq', 'batch'))
- new_moment_two: float32 [2560, 2560], P(('seq', 'batch'))
All inputs are finite; a program needn't handle non-finite values.
Results may differ from a plain program's by a relative error of at most 0.01.
Values may be sent and summed in bfloat16 or wider, within the bound.
A program may use at most 128 MiB of HBM per device.

v0:
```python
import jax
import jax.numpy as jnp
from jax import lax
from jax.sharding import PartitionSpec as P

DIN = 2560
DOUT = 2560
GRAD_BLOCKS = 4
STEP = 10


def on_device(attn_out, out_grad, master, moment_one, moment_two):
    shard_weight = master.astype(jnp.bfloat16)
    projected = lax.dot_general(
        out_grad,
        lax.all_gather(shard_weight, ("seq", "batch"), axis=0, tiled=True),
        (((1,), (1,)), ((), ())),
        preferred_element_type=jnp.float32,
    )
    input_grad = projected.astype(jnp.bfloat16)
    block_width = out_grad.shape[1] // GRAD_BLOCKS
    grad_parts = []
    for block in range(GRAD_BLOCKS):
        grad_cols = out_grad[:, block * block_width : (block + 1) * block_width]
        seq_summed = lax.psum_scatter(
            lax.dot_general(
                attn_out, grad_cols, (((0,), (0,)), ((), ())), preferred_element_type=jnp.float32
            ).astype(jnp.bfloat16),
            "seq",
            scatter_dimension=0,
            tiled=True,
        )
        grad_parts.append(
            lax.psum_scatter(seq_summed, "batch", scatter_dimension=0, tiled=True).astype(
                jnp.float32
            )
        )
    weight_grad = jnp.concatenate(grad_parts, axis=1)
    squares = lax.psum(jnp.sum(weight_grad * weight_grad), ("seq", "batch"))
    grad_norm = jnp.sqrt(squares) + 1e-06
    limit = jnp.sqrt(jnp.float32(DIN * DOUT))
    clipped = weight_grad * jnp.minimum(jnp.float32(1.0), limit / grad_norm)
    new_one = 0.9 * moment_one + 0.1 * clipped
    new_two = 0.999 * moment_two + 0.001 * clipped * clipped
    first_hat = new_one / (1.0 - 0.9**STEP)
    second_hat = new_two / (1.0 - 0.999**STEP)
    new_master = master - 0.01 * (first_hat / (jnp.sqrt(second_hat) + 1e-08) + 0.1 * master)
    return (input_grad, new_master, new_one, new_two)


def solution(mesh):
    return jax.shard_map(
        on_device,
        mesh=mesh,
        in_specs=(
            P(("seq", "batch"), None),
            P(("seq", "batch"), None),
            P(("seq", "batch"), None),
            P(("seq", "batch"), None),
            P(("seq", "batch"), None),
        ),
        out_specs=(
            P(("seq", "batch"), None),
            P(("seq", "batch"), None),
            P(("seq", "batch"), None),
            P(("seq", "batch"), None),
        ),
        check_vma=False,
    )
```

profile of v0, /device:TPU:0, one launch (start us, length us, event | category | flops | bytes accessed | tf_op | source)
XLA Modules:
  0.0 499.1 jit_solution(9596694744249055600)
XLA Ops:
  7.2 0.0 reduce-scatter.13.cloned.1.call-start
  7.2 1.7 copy-done
  8.9 5.1 %convolution_convert_fusion.2 = bf16[2560,640]{1,0:T(8,128)(2,1)} fusion(bf16[512,2560]{1,0:T(8,128)(2,1)S(1)} %copy-done, bf16[512,2560]{1,0:T(8,128)(2,1)} %param.6), kind=kOutput, calls=%fused_computation.2 | convolution fusion | flops 1679360000 | bytes 6553600 | tf_op jit(solution)/shard_map/dot_general | solution.py:26
  14.0 0.0 reduce-scatter.9.cloned.1.call-start
  14.1 5.1 %convolution_convert_fusion.3 = bf16[2560,640]{1,0:T(8,128)(2,1)} fusion(bf16[512,2560]{1,0:T(8,128)(2,1)S(1)} %copy-done, bf16[512,2560]{1,0:T(8,128)(2,1)} %param.6), kind=kOutput, calls=%fused_computation.3 | convolution fusion | flops 1679360000 | bytes 6553600 | tf_op jit(solution)/shard_map/dot_general | solution.py:26
  19.1 0.0 reduce-scatter.21.cloned.1.call-start
  19.2 5.0 %convolution_convert_fusion = bf16[2560,640]{1,0:T(8,128)(2,1)} fusion(bf16[512,2560]{1,0:T(8,128)(2,1)S(1)} %copy-done, bf16[512,2560]{1,0:T(8,128)(2,1)} %param.6), kind=kOutput, calls=%fused_computation | convolution fusion | flops 1679360000 | bytes 6553600 | tf_op jit(solution)/shard_map/dot_general | solution.py:26
  24.2 0.0 reduce-scatter.17.cloned.1.call-start
  24.3 5.1 %convolution_convert_fusion.1 = bf16[2560,640]{1,0:T(8,128)(2,1)} fusion(bf16[512,2560]{1,0:T(8,128)(2,1)S(1)} %copy-done, bf16[512,2560]{1,0:T(8,128)(2,1)} %param.6), kind=kOutput, calls=%fused_computation.1 | convolution fusion | flops 1679360000 | bytes 6553600 | tf_op jit(solution)/shard_map/dot_general | solution.py:26
  29.4 0.0 reduce-scatter.15.cloned.1.call-start
  29.4 32.5 %reduce-scatter.13.cloned.1.call-done = bf16[640,640]{1,0:T(8,128)(2,1)} async-done(((bf16[2560,640]{1,0:T(8,128)(2,1)}), bf16[640,640]{1,0:T(8,128)(2,1)}) %reduce-scatter.13.cloned.1.call-update) | async-done | bytes 819216 | tf_op jit(solution)/shard_map/reduce_scatter | solution.py:25
  62.0 48.0 %reduce-scatter.9.cloned.1.call-done = bf16[640,640]{1,0:T(8,128)(2,1)} async-done(((bf16[2560,640]{1,0:T(8,128)(2,1)}), bf16[640,640]{1,0:T(8,128)(2,1)}) %reduce-scatter.9.cloned.1.call-update) | async-done | bytes 819216 | tf_op jit(solution)/shard_map/reduce_scatter | solution.py:25
  110.0 48.0 %reduce-scatter.21.cloned.1.call-done = bf16[640,640]{1,0:T(8,128)(2,1)} async-done(((bf16[2560,640]{1,0:T(8,128)(2,1)}), bf16[640,640]{1,0:T(8,128)(2,1)}) %reduce-scatter.21.cloned.1.call-update) | async-done | bytes 819216 | tf_op jit(solution)/shard_map/reduce_scatter | solution.py:25
  158.1 47.8 %reduce-scatter.17.cloned.1.call-done = bf16[640,640]{1,0:T(8,128)(2,1)} async-done(((bf16[2560,640]{1,0:T(8,128)(2,1)}), bf16[640,640]{1,0:T(8,128)(2,1)}) %reduce-scatter.17.cloned.1.call-update) | async-done | bytes 819216 | tf_op jit(solution)/shard_map/reduce_scatter | solution.py:25
  205.9 0.0 all-gather.2.cloned.1.call-start
  206.0 34.2 %reduce-scatter.15.cloned.1.call-done = bf16[80,640]{1,0:T(8,128)(2,1)} async-done(((bf16[640,640]{1,0:T(8,128)(2,1)}), bf16[80,640]{1,0:T(8,128)(2,1)}) %reduce-scatter.15.cloned.1.call-update) | async-done | bytes 102416 | tf_op jit(solution)/shard_map/reduce_scatter | solution.py:34
  240.2 32.5 %reduce-scatter.11.cloned.1.call-done = bf16[80,640]{1,0:T(8,128)(2,1)} async-done(((bf16[640,640]{1,0:T(8,128)(2,1)}), bf16[80,640]{1,0:T(8,128)(2,1)}) %reduce-scatter.11.cloned.1.call-update) | async-done | bytes 102416 | tf_op jit(solution)/shard_map/reduce_scatter | solution.py:34
  272.6 32.6 %reduce-scatter.23.cloned.1.call-done = bf16[80,640]{1,0:T(8,128)(2,1)} async-done(((bf16[640,640]{1,0:T(8,128)(2,1)}), bf16[80,640]{1,0:T(8,128)(2,1)}) %reduce-scatter.23.cloned.1.call-update) | async-done | bytes 102416 | tf_op jit(solution)/shard_map/reduce_scatter | solution.py:34
  305.2 32.6 %reduce-scatter.19.cloned.1.call-done = bf16[80,640]{1,0:T(8,128)(2,1)} async-done(((bf16[640,640]{1,0:T(8,128)(2,1)}), bf16[80,640]{1,0:T(8,128)(2,1)}) %reduce-scatter.19.cloned.1.call-update) | async-done | bytes 102416 | tf_op jit(solution)/shard_map/reduce_scatter | solution.py:34
  337.8 1.9 fusion.2
  339.7 38.1 %psum.7 = f32[]{:T(128)} all-reduce(f32[]{:T(128)} %fusion.2), channel_id=1, replica_groups=mesh['seq'=4,'batch'=8] {'seq','batch'}, use_global_device_ids=true, to_apply=%region_9.0 | all-reduce | flops 1 | bytes 8 | tf_op jit(solution)/shard_map/psum | solution.py:39
  378.5 3.6 multiply_subtract_fusion
  382.1 98.5 %all-gather.2.cloned.1.call-done = bf16[2560,2560]{1,0:T(8,128)(2,1)} async-done(((bf16[80,2560]{1,0:T(8,128)(2,1)}), bf16[2560,2560]{1,0:T(8,128)(2,1)}) %all-gather.2.cloned.1.call-update) | async-done | bytes 13107216 | tf_op jit(solution)/shard_map/all_gather | solution.py:16
  480.7 11.9 %convolution_convert_fusion.4 = bf16[512,2560]{1,0:T(8,128)(2,1)} fusion(bf16[512,2560]{1,0:T(8,128)(2,1)} %param.6, bf16[2560,2560]{1,0:T(8,128)(2,1)} %all-gather.2.cloned.1.call-done), kind=kOutput, calls=%fused_computation.4 | convolution fusion | flops 6712197120 | bytes 18350080 | tf_op jit(solution)/shard_map/dot_general | solution.py:14
  (15 shorter events, 0.3 us)
Async XLA Ops:
  7.2 1.7 copy-start
  7.2 54.7 %reduce-scatter.13.cloned.1.call-start = ((), (), s32[]{:S(2)}) async-start(), calls=%async_computation.11 | async-start | bytes 4096000 | tf_op jit(solution)/shard_map/reduce_scatter | solution.py:25
  14.0 95.9 %reduce-scatter.9.cloned.1.call-start = ((), (), s32[]{:S(2)}) async-start(), calls=%async_computation.9 | async-start | bytes 4096000 | tf_op jit(solution)/shard_map/reduce_scatter | solution.py:25
  19.1 138.8 %reduce-scatter.21.cloned.1.call-start = ((), (), s32[]{:S(2)}) async-start(), calls=%async_computation.15 | async-start | bytes 4096000 | tf_op jit(solution)/shard_map/reduce_scatter | solution.py:25
  24.2 181.7 %reduce-scatter.17.cloned.1.call-start = ((), (), s32[]{:S(2)}) async-start(), calls=%async_computation.13 | async-start | bytes 4096000 | tf_op jit(solution)/shard_map/reduce_scatter | solution.py:25
  29.4 349.1 %copy-start.1 = (f32[80,2560]{1,0:T(8,128)S(1)}, f32[80,2560]{1,0:T(8,128)}, u32[]{:S(2)}) copy-start(f32[80,2560]{1,0:T(8,128)} %param.7) | copy-start | bytes 2457604
  29.4 210.8 %reduce-scatter.15.cloned.1.call-start = ((), (), s32[]{:S(2)}) async-start(), calls=%async_computation.12 | async-start | bytes 921600 | tf_op jit(solution)/shard_map/reduce_scatter | solution.py:34
  61.9 210.7 %reduce-scatter.11.cloned.1.call-start = ((), (), s32[]{:S(2)}) async-start(), calls=%async_computation.10 | async-start | bytes 921600 | tf_op jit(solution)/shard_map/reduce_scatter | solution.py:34
  110.0 195.3 %reduce-scatter.23.cloned.1.call-start = ((), (), s32[]{:S(2)}) async-start(), calls=%async_computation.16 | async-start | bytes 921600 | tf_op jit(solution)/shard_map/reduce_scatter | solution.py:34
  158.0 179.8 %reduce-scatter.19.cloned.1.call-start = ((), (), s32[]{:S(2)}) async-start(), calls=%async_computation.14 | async-start | bytes 921600 | tf_op jit(solution)/shard_map/reduce_scatter | solution.py:34
  205.9 274.8 %all-gather.2.cloned.1.call-start = ((), (), s32[]{:S(2)}) async-start(), calls=%async_computation.8 | async-start | bytes 13516800 | tf_op jit(solution)/shard_map/all_gather | solution.py:16
Sparse Core Ops, SparseCore 0:
  14.1 47.7 reduce-scatter.12
  64.9 44.9 reduce-scatter.8
  113.0 44.9 reduce-scatter.20
  160.9 44.9 reduce-scatter.16
  208.0 32.0 reduce-scatter.14
  242.3 30.2 reduce-scatter.10
  274.9 30.2 reduce-scatter.22
  307.5 30.2 reduce-scatter.18
  382.3 98.3 all-gather.1
where the time goes:
time: 500 us; the launch traced here: 499 us
  waiting for transfers between devices  407 us (81%)
  blocking collectives  38.1 us (8%)
  matrix products  32.1 us (6%)
  between operations  14.6 us (3%)
  other arithmetic  5.46 us (1%)
    reduce_scatter x4, waiting for transfers between devices, on_device(): lax.psum_scatter(lax.dot_general(attn_out, grad_cols, (((0,), (0,)), ((),...  176 us
    reduce_scatter x4, waiting for transfers between devices, on_device(): lax.psum_scatter(seq_summed, 'batch', scatter_dimension=0, tiled=True)  132 us
    all_gather x1, waiting for transfers between devices, on_device(): lax.all_gather(shard_weight, ('seq', 'batch'), axis=0, tiled=True)  98.5 us
    psum x1, blocking collectives, on_device(): squares = lax.psum(jnp.sum(weight_grad * weight_grad), ('seq', 'batch'))  38.1 us
    dot_general x4, matrix products, on_device(): lax.dot_general(attn_out, grad_cols, (((0,), (0,)), ((), ())), preferred_...  20.2 us
    dot_general x1, matrix products, on_device(): lax.dot_general(out_grad, lax.all_gather(shard_weight, ('seq', 'batch'),...  11.9 us
  transfers between devices with their start and end apart: 9, of which 9 were waited for; matrix products, arithmetic and copies ran while one was open for 3% of the time, Pallas kernels for 0%

commit v1 on v0

v1 whole, which is shorter than its diff:
```python
import functools
import jax
import jax.numpy as jnp
from jax import lax
from jax.experimental import pallas as pl
from jax.experimental.pallas import tpu as pltpu
from jax.sharding import PartitionSpec as P

GRAD_BLOCKS = 4
STEP = 10
MESH = pl.DeviceIdType.MESH
F32 = jnp.float32
BF16 = jnp.bfloat16


def kernel(nb, attn_ref, og_ref, w_ref, ig_ref, gw_ref, sq_ref,
           rx_attn, rx_og, tbuf, attn_t, wg, g, r1a, r1b, r2, t2, pz, rz, sqs,
           x_s, x_r, z_s, z_r, p_s, p_r, d_s, d_r, c_s, c_r,
           s1_s, s1_r, s2_s, s2_r, rz_s, rz_r, q_s, q_r):
    ns = 4
    nz = nb // 2
    tok, din = attn_ref.shape
    dout = og_ref.shape[1]
    r = w_ref.shape[0]
    half = dout // 2
    block = nb * r
    seq = lax.axis_index("seq")
    batch = lax.axis_index("batch")
    z = batch // 2
    core = batch % 2
    hi = seq // 2
    lo = seq % 2
    sh = (1 - hi) * 2 + lo
    sl = hi * 2 + (1 - lo)
    sd = (1 - hi) * 2 + (1 - lo)
    hi_dev = (sh, batch)
    lo_dev = (sl, batch)
    core_dev = (seq, z * 2 + 1 - core)
    cols_a = pl.ds(0, half)
    cols_b = pl.ds(half, half)

    def other(i):
        f = lax.rem(seq * nb + batch + i, ns * nb)
        return (f // nb, lax.rem(f, nb))

    barrier = pltpu.get_barrier_semaphore()

    def greet(i, carry):
        pl.semaphore_signal(barrier, inc=1, device_id=other(i), device_id_type=MESH)
        return carry

    lax.fori_loop(1, ns * nb, greet, 0)
    pl.semaphore_wait(barrier, ns * nb - 1)

    pending = []

    def remote(src, dst, ssem, rsem, dev):
        c = pltpu.make_async_remote_copy(
            src_ref=src, dst_ref=dst, send_sem=ssem, recv_sem=rsem,
            device_id=dev, device_id_type=MESH)
        c.start()
        pending.append(c)
        return c

    def zk(k):
        return lax.rem(z + nz - k, nz)

    def wrows(s, zz):
        return pl.ds(pl.multiple_of((s * nb + zz * 2 + core) * r, 16), r)

    def shard(k):
        return w_ref if k == 0 else wg.at[wrows(seq, zk(k))]

    own = wrows(seq, z)
    zc, hc, lc, dac, dbc, cc = {}, {}, {}, {}, {}, {}

    def plane_send(k):
        rows = wrows(seq, zk(k))
        hc[k] = remote(shard(k), wg.at[rows], p_s.at[2 * k], p_r.at[2 * k], hi_dev)
        lc[k] = remote(shard(k), wg.at[rows], p_s.at[2 * k + 1], p_r.at[2 * k + 1], lo_dev)

    def core_send(k, j, s):
        rows = wrows(s, zk(k))
        src = w_ref if (k == 0 and j == 0) else wg.at[rows]
        i = 4 * k + j
        cc[i] = remote(src, wg.at[rows], c_s.at[i], c_r.at[i], core_dev)

    def z_arrive(k):
        zc[k].wait_recv()
        plane_send(k)
        core_send(k, 0, seq)

    def plane_arrive(k):
        hc[k].wait_recv()
        v = wg.at[wrows(sh, zk(k)), cols_a]
        dac[k] = remote(v, v, d_s.at[2 * k], d_r.at[2 * k], lo_dev)
        lc[k].wait_recv()
        v = wg.at[wrows(sl, zk(k)), cols_b]
        dbc[k] = remote(v, v, d_s.at[2 * k + 1], d_r.at[2 * k + 1], hi_dev)
        core_send(k, 1, sh)
        core_send(k, 2, sl)

    def diag_arrive(k):
        dac[k].wait_recv()
        dbc[k].wait_recv()
        core_send(k, 3, sd)

    xa = remote(attn_ref, rx_attn, x_s.at[0], x_r.at[0], core_dev)
    plane_send(0)
    for k in range(1, nz):
        dev = (seq, lax.rem(z + k, nz) * 2 + core)
        zc[k] = remote(w_ref, wg.at[own], z_s.at[k], z_r.at[k], dev)
    xo = remote(og_ref, rx_og, x_s.at[1], x_r.at[1], core_dev)
    core_send(0, 0, seq)
    wg[own, :] = w_ref[...]

    def transpose_in(src, koff):
        for s in range(ns):
            tbuf[...] = src[:, s * block:(s + 1) * block].T
            for zz in range(nz):
                part = tbuf[pl.ds(pl.multiple_of((zz * 2 + core) * r, 16), r), :]
                attn_t[pl.ds((s * nz + zz) * r, r), pl.ds(koff, tok)] = part

    tile = 256 if dout % 256 == 0 and din % 256 == 0 else 128
    ntile = dout // tile

    def grad_tiles(first, last):
        def body(i, carry):
            c = pl.ds(pl.multiple_of(i * tile, tile), tile)
            acc = jnp.dot(attn_t[:, :tok], og_ref[:, c], preferred_element_type=F32)
            acc += jnp.dot(attn_t[:, tok:], rx_og[:, c], preferred_element_type=F32)
            g[:, c] = acc.astype(BF16)
            return carry
        lax.fori_loop(first, last, body, 0)

    transpose_in(attn_ref, 0)
    if nz > 1:
        z_arrive(1)
    xa.wait_recv()
    transpose_in(rx_attn, tok)
    plane_arrive(0)
    xo.wait_recv()
    for k in range(1, nz):
        grad_tiles((k - 1) * ntile // (nz - 1), k * ntile // (nz - 1))
        if k + 1 < nz:
            z_arrive(k + 1)
        if k < nz - 1:
            plane_arrive(k)

    def grows(s, i):
        return pl.ds(pl.multiple_of((s * nz + lax.rem(z + 1 + i, nz)) * r, 16), r)

    def rr(i):
        return pl.ds(i * r, r)

    s1, s2 = {}, {}

    def stage1(i):
        s1[i] = [
            remote(g.at[grows(sd, i), cols_a], r1a.at[rr(2 * i + 1)], s1_s.at[4 * i], s1_r.at[4 * i], hi_dev),
            remote(g.at[grows(sd, i), cols_b], r1b.at[rr(2 * i + 1)], s1_s.at[4 * i + 1], s1_r.at[4 * i + 1], lo_dev),
            remote(g.at[grows(sh, i), cols_a], r1a.at[rr(2 * i)], s1_s.at[4 * i + 2], s1_r.at[4 * i + 2], hi_dev),
            remote(g.at[grows(sl, i), cols_b], r1b.at[rr(2 * i)], s1_s.at[4 * i + 3], s1_r.at[4 * i + 3], lo_dev),
        ]

    def stage2(i):
        s1[i][0].wait_recv()
        t2[rr(i), cols_a] = (g[grows(sl, i), cols_a].astype(F32) + r1a[rr(2 * i + 1), :].astype(F32)).astype(BF16)
        ca = remote(t2.at[rr(i), cols_a], r2.at[rr(i), cols_a], s2_s.at[2 * i], s2_r.at[2 * i], lo_dev)
        s1[i][1].wait_recv()
        t2[rr(i), cols_b] = (g[grows(sh, i), cols_b].astype(F32) + r1b[rr(2 * i + 1), :].astype(F32)).astype(BF16)
        cb = remote(t2.at[rr(i), cols_b], r2.at[rr(i), cols_b], s2_s.at[2 * i + 1], s2_r.at[2 * i + 1], hi_dev)
        s2[i] = [ca, cb]

    zsum = {}

    def stage3(i):
        for c in (s1[i][2], s1[i][3], s2[i][0], s2[i][1]):
            c.wait_recv()
        for cols, r1 in ((cols_a, r1a), (cols_b, r1b)):
            v = g[grows(seq, i), cols].astype(F32) + r1[rr(2 * i), :].astype(F32) + r2[rr(i), cols].astype(F32)
            if i == nz - 1:
                gw_ref[:, cols] = v
            else:
                pz[rr(i), cols] = v.astype(BF16)
        if i < nz - 1:
            dev = (seq, lax.rem(z + 1 + i, nz) * 2 + core)
            zsum[i] = remote(pz.at[rr(i)], rz.at[rr(i)], rz_s.at[i], rz_r.at[i], dev)

    stage1(0)
    if nz > 1:
        plane_arrive(nz - 1)
    for k in range(nz):
        diag_arrive(k)
        if k == 0 and nz > 1:
            stage1(1)

    def input_tiles(first, last):
        def body(i, carry):
            c = pl.ds(pl.multiple_of(i * tile, tile), tile)
            v = lax.dot_general(og_ref[...], wg[c, :], (((1,), (1,)), ((), ())), preferred_element_type=F32)
            ig_ref[:, c] = v.astype(BF16)
            return carry
        lax.fori_loop(first, last, body, 0)

    itile = din // tile
    stage2(0)
    for i in range(4 * nz):
        cc[i].wait_recv()
    for i in range(nz):
        input_tiles(i * itile // nz, (i + 1) * itile // nz)
        if i + 2 < nz:
            stage1(i + 2)
        if i + 1 < nz:
            stage2(i + 1)
        stage3(i)
    for i in range(nz - 1):
        zsum[i].wait_recv()
        gw_ref[...] += rz[rr(i), :].astype(F32)

    v = gw_ref[...]
    part = jnp.sum((v * v).reshape(r // 8, 8, dout), axis=0)
    acc = part[:, :128]
    for i in range(1, dout // 128):
        acc += part[:, i * 128:(i + 1) * 128]
    sqs[0] = acc

    def q_copy(i):
        return pltpu.make_async_remote_copy(
            src_ref=sqs.at[0], dst_ref=sqs.at[i], send_sem=q_s.at[i], recv_sem=q_r.at[i],
            device_id=other(i), device_id_type=MESH)

    def q_start(i, carry):
        q_copy(i).start()
        return carry

    def q_wait(i, carry):
        q_copy(i).wait()
        return carry

    lax.fori_loop(1, ns * nb, q_start, 0)
    lax.fori_loop(1, ns * nb, q_wait, 0)
    total = sqs[0]
    for i in range(1, ns * nb):
        total += sqs[i]
    sq_ref[...] = total
    for c in pending:
        c.wait_send()


def fused(attn_out, out_grad, shard_weight, ns, nb):
    tok, din = attn_out.shape
    dout = out_grad.shape[1]
    r = shard_weight.shape[0]
    nz = nb // 2
    n = ns * nb
    dma = lambda k: pltpu.SemaphoreType.DMA((k,))
    vm = pl.BlockSpec(memory_space=pltpu.VMEM)
    pairs = [2, nz, 2 * nz, 2 * nz, 4 * nz, 4 * nz, 2 * nz, nz, n]
    return pl.pallas_call(
        functools.partial(kernel, nb),
        out_shape=(
            jax.ShapeDtypeStruct((tok, din), BF16),
            jax.ShapeDtypeStruct((r, dout), F32),
            jax.ShapeDtypeStruct((8, 128), F32),
        ),
        in_specs=[vm] * 3,
        out_specs=(vm,) * 3,
        scratch_shapes=[
            pltpu.VMEM((tok, din), BF16),
            pltpu.VMEM((tok, dout), BF16),
            pltpu.VMEM((nb * r, tok), BF16),
            pltpu.VMEM((din // 2, 2 * tok), BF16),
            pltpu.VMEM((din, dout), BF16),
            pltpu.VMEM((din // 2, dout), BF16),
            pltpu.VMEM((2 * nz * r, dout // 2), BF16),
            pltpu.VMEM((2 * nz * r, dout // 2), BF16),
            pltpu.VMEM((nz * r, dout), BF16),
            pltpu.VMEM((nz * r, dout), BF16),
            pltpu.VMEM((nz * r, dout), BF16),
            pltpu.VMEM((nz * r, dout), BF16),
            pltpu.VMEM((n, 8, 128), F32),
        ] + [dma(k) for k in pairs for _ in range(2)],
        compiler_params=pltpu.CompilerParams(
            collective_id=0, has_side_effects=True, vmem_limit_bytes=66_000_000),
    )(attn_out, out_grad, shard_weight)


def plain(attn_out, out_grad, shard_weight):
    projected = lax.dot_general(
        out_grad,
        lax.all_gather(shard_weight, ("seq", "batch"), axis=0, tiled=True),
        (((1,), (1,)), ((), ())),
        preferred_element_type=F32,
    )
    width = out_grad.shape[1] // GRAD_BLOCKS
    parts = []
    for b in range(GRAD_BLOCKS):
        d = lax.dot_general(
            attn_out, out_grad[:, b * width:(b + 1) * width],
            (((0,), (0,)), ((), ())), preferred_element_type=F32).astype(BF16)
        d = lax.psum_scatter(d, "seq", scatter_dimension=0, tiled=True)
        parts.append(lax.psum_scatter(d, "batch", scatter_dimension=0, tiled=True).astype(F32))
    weight_grad = jnp.concatenate(parts, axis=1)
    squares = lax.psum(jnp.sum(weight_grad * weight_grad), ("seq", "batch"))
    return projected.astype(BF16), weight_grad, squares


def on_device(ns, nb, attn_out, out_grad, master, moment_one, moment_two):
    shard_weight = master.astype(BF16)
    r, dout = master.shape
    din = attn_out.shape[1]
    if ns == 4 and nb % 2 == 0 and r % 16 == 0 and (nb * r) % 128 == 0 and dout % 256 == 0:
        input_grad, weight_grad, sq = fused(attn_out, out_grad, shard_weight, ns, nb)
        squares = jnp.sum(sq)
    else:
        input_grad, weight_grad, squares = plain(attn_out, out_grad, shard_weight)
    grad_norm = jnp.sqrt(squares) + 1e-06
    limit = jnp.sqrt(jnp.float32(din * dout))
    clipped = weight_grad * jnp.minimum(jnp.float32(1.0), limit / grad_norm)
    new_one = 0.9 * moment_one + 0.1 * clipped
    new_two = 0.999 * moment_two + 0.001 * clipped * clipped
    first_hat = new_one / (1.0 - 0.9**STEP)
    second_hat = new_two / (1.0 - 0.999**STEP)
    new_master = master - 0.01 * (first_hat / (jnp.sqrt(second_hat) + 1e-08) + 0.1 * master)
    return (input_grad, new_master, new_one, new_two)


def solution(mesh):
    spec = P(("seq", "batch"), None)
    return jax.shard_map(
        functools.partial(on_device, mesh.shape["seq"], mesh.shape["batch"]),
        mesh=mesh,
        in_specs=(spec,) * 5,
        out_specs=(spec,) * 4,
        check_vma=False,
    )
```

time: 500 us -> 156 us (0.31)
  waiting for transfers between devices: 407 us -> 0 us
  Pallas kernels: 0 us -> 146 us
  blocking collectives: 38.1 us -> 0 us
  matrix products: 32.1 us -> 0 us
  between operations: 14.6 us -> 1.39 us
    reduce_scatter x8 -> x0, waiting for transfers between devices: 308 us -> none  [the longest x4 176 us: on_device(): lax.psum_scatter(lax.dot_general(attn_out, grad_cols, (((0,), (0,)), ((),...]
    pallas_call x0 -> x1, Pallas kernels: none -> 146 us  [fused(): pl.pallas_call(functools.partial(kernel, nb), out_shape=(jax.ShapeDtypeSt...]
    all_gather x1 -> x0, waiting for transfers between devices: 98.5 us -> none  [on_device(): lax.all_gather(shard_weight, ('seq', 'batch'), axis=0, tiled=True)]
    psum x1 -> x0, blocking collectives: 38.1 us -> none  [on_device(): squares = lax.psum(jnp.sum(weight_grad * weight_grad), ('seq', 'batch'))]
    dot_general x5 -> x0, matrix products: 32.1 us -> none  [the longest x4 20.2 us: on_device(): lax.dot_general(attn_out, grad_cols, (((0,), (0,)), ((), ())), preferred_...]
  transfers between devices with their start and end apart: 9 -> 0, of which waited for: 9 -> 0; matrix products, arithmetic and copies ran while one was open for 3% -> 0% of each run, Pallas kernels for 0% -> 0%
where the time goes in v1:
time: 156 us
  Pallas kernels  146 us (94%)
  other arithmetic  6.88 us (4%)
    pallas_call x1, Pallas kernels, fused(): pl.pallas_call(functools.partial(kernel, nb), out_shape=(jax.ShapeDtypeSt...  146 us
    sub x1, other arithmetic, on_device(): master - 0.01 * (first_hat / (jnp.sqrt(second_hat) + 1e-08) + 0.1 * master)  3.65 us

profile of v1, /device:TPU:0, one launch (start us, length us, event | category | flops | bytes accessed | tf_op | source)
XLA Modules:
  0.0 155.5 jit_solution(16555169006744493451)
XLA Ops:
  0.6 1.9 %convert_element_type.3.w_ref = bf16[80,2560]{1,0:T(8,128)(2,1)} convert(f32[80,2560]{1,0:T(8,128)} %param.7) | non-fusion elementwise | flops 204800 | bytes 1228800 | tf_op jit(solution)/shard_map/convert_element_type | solution.py:310
  2.6 0.0 copy-start
  2.6 145.7 %shard_map.84 = (bf16[512,2560]{1,0:T(8,128)(2,1)}, f32[80,2560]{1,0:T(8,128)}, f32[8,128]{1,0:T(8,128)}) custom-call(bf16[512,2560]{1,0:T(8,128)(2,1)} %attn_ref.1, bf16[512,2560]{1,0:T(8,128)(2,1)} %og_ref.1, bf16[80,2560]{1,0:T(8,128)(2,1)} %convert_element_type.3.w_ref), custom_call_target="tpu_custom_call" | custom-call | tf_op jit(solution)/shard_map/pallas_call | solution.py:260
  148.3 1.3 reduce_sum.9
  150.3 0.0 copy-done
  150.3 0.0 copy-start.1
  150.4 3.7 %multiply_subtract_fusion = (f32[80,2560]{1,0:T(8,128)}, f32[80,2560]{1,0:T(8,128)}, f32[80,2560]{1,0:T(8,128)}) fusion(f32[80,2560]{1,0:T(8,128)S(1)} %copy-done, f32[80,2560]{1,0:T(8,128)} %get-tuple-element.8, f32[]{:T(128)S(6)} %min_shard_map.3, f32[80,2560]{1,0:T(8,128)} %param.8, f32[80,2560]{1,0:T(8,128)} %param.9), kind=kLoop, calls=%fused_computation.2 | loop fusion | flops 3276800 | bytes 5734404 | tf_op jit(solution)/shard_map/sub | solution.py:325
  154.0 0.0 copy-done.1
  154.0 1.5 copy.10
Async XLA Ops:
  2.6 147.8 %copy-start = (f32[80,2560]{1,0:T(8,128)S(1)}, f32[80,2560]{1,0:T(8,128)}, u32[]{:S(2)}) copy-start(f32[80,2560]{1,0:T(8,128)} %param.7) | copy-start | bytes 2457604
  150.3 3.7 %copy-start.1 = (bf16[512,2560]{1,0:T(8,128)(2,1)S(1)}, bf16[512,2560]{1,0:T(8,128)(2,1)}, u32[]{:S(2)}) copy-start(bf16[512,2560]{1,0:T(8,128)(2,1)} %get-tuple-element.17) | copy-start | bytes 7864324

commit v2 on v1

--- a/solution.py
+++ b/solution.py
@@ -13,8 +13,8 @@
 BF16 = jnp.bfloat16
 
 
-def kernel(nb, attn_ref, og_ref, w_ref, ig_ref, gw_ref, sq_ref,
-           rx_attn, rx_og, tbuf, attn_t, wg, g, r1a, r1b, r2, t2, pz, rz, sqs,
+def kernel(nb, attn_hbm, og_hbm, w_ref, ig_ref, gw_ref, sq_ref,
+           attn_ref, og_ref, l_s, rx_attn, rx_og, tbuf, attn_t, wg, g, r1a, r1b, r2, t2, pz, rz, sqs,
            x_s, x_r, z_s, z_r, p_s, p_r, d_s, d_r, c_s, c_r,
            s1_s, s1_r, s2_s, s2_r, rz_s, rz_r, q_s, q_r):
     ns = 4
@@ -43,6 +43,10 @@
         f = lax.rem(seq * nb + batch + i, ns * nb)
         return (f // nb, lax.rem(f, nb))
 
+    la = pltpu.make_async_copy(attn_hbm, attn_ref, l_s.at[0])
+    la.start()
+    lg = pltpu.make_async_copy(og_hbm, og_ref, l_s.at[1])
+    lg.start()
     barrier = pltpu.get_barrier_semaphore()
 
     def greet(i, carry):
@@ -62,8 +66,35 @@
         pending.append(c)
         return c
 
-    def zk(k):
-        return lax.rem(z + nz - k, nz)
+    near = jnp.minimum(z, nz - 1 - z)
+
+    def zk(t):
+        if t == 0:
+            return z
+        both = t <= 2 * near
+        dist = jnp.where(both, (t + 1) // 2, t - near)
+        above = jnp.where(both, t % 2, jnp.where(z < nz - 1 - z, 1, 0))
+        return z + dist * (2 * above - 1)
+
+    def z_copy(t, up):
+        src = zk(t)
+        to = jnp.minimum(z + 1, nz - 1) if up else jnp.maximum(z - 1, 0)
+        return pltpu.make_async_remote_copy(
+            src_ref=shard(t), dst_ref=wg.at[wrows(seq, src)],
+            send_sem=z_s.at[nz * up + src], recv_sem=z_r.at[src],
+            device_id=(seq, to * 2 + core), device_id_type=MESH)
+
+    def z_pass(t, up):
+        src = zk(t)
+        if up:
+            return jnp.logical_and(src <= z, z < nz - 1)
+        return jnp.logical_and(src >= z, z > 0)
+
+    def z_each(t, act):
+        for up in (0, 1):
+            @pl.when(z_pass(t, up))
+            def _():
+                act(z_copy(t, up))
 
     def wrows(s, zz):
         return pl.ds(pl.multiple_of((s * nb + zz * 2 + core) * r, 16), r)
@@ -72,7 +103,7 @@
         return w_ref if k == 0 else wg.at[wrows(seq, zk(k))]
 
     own = wrows(seq, z)
-    zc, hc, lc, dac, dbc, cc = {}, {}, {}, {}, {}, {}
+    hc, lc, dac, dbc, cc = {}, {}, {}, {}, {}
 
     def plane_send(k):
         rows = wrows(seq, zk(k))
@@ -86,7 +117,8 @@
         cc[i] = remote(src, wg.at[rows], c_s.at[i], c_r.at[i], core_dev)
 
     def z_arrive(k):
-        zc[k].wait_recv()
+        z_copy(k, 0).wait_recv()
+        z_each(k, lambda c: c.start())
         plane_send(k)
         core_send(k, 0, seq)
 
@@ -105,12 +137,10 @@
         dbc[k].wait_recv()
         core_send(k, 3, sd)
 
-    xa = remote(attn_ref, rx_attn, x_s.at[0], x_r.at[0], core_dev)
+    xa = remote(attn_hbm, rx_attn, x_s.at[0], x_r.at[0], core_dev)
     plane_send(0)
-    for k in range(1, nz):
-        dev = (seq, lax.rem(z + k, nz) * 2 + core)
-        zc[k] = remote(w_ref, wg.at[own], z_s.at[k], z_r.at[k], dev)
-    xo = remote(og_ref, rx_og, x_s.at[1], x_r.at[1], core_dev)
+    z_each(0, lambda c: c.start())
+    xo = remote(og_hbm, rx_og, x_s.at[1], x_r.at[1], core_dev)
     core_send(0, 0, seq)
     wg[own, :] = w_ref[...]
 
@@ -133,6 +163,7 @@
             return carry
         lax.fori_loop(first, last, body, 0)
 
+    la.wait()
     transpose_in(attn_ref, 0)
     if nz > 1:
         z_arrive(1)
@@ -140,6 +171,7 @@
     transpose_in(rx_attn, tok)
     plane_arrive(0)
     xo.wait_recv()
+    lg.wait()
     for k in range(1, nz):
         grad_tiles((k - 1) * ntile // (nz - 1), k * ntile // (nz - 1))
         if k + 1 < nz:
@@ -246,6 +278,8 @@
     sq_ref[...] = total
     for c in pending:
         c.wait_send()
+    for t in range(nz):
+        z_each(t, lambda c: c.wait_send())
 
 
 def fused(attn_out, out_grad, shard_weight, ns, nb):
@@ -256,7 +290,7 @@
     n = ns * nb
     dma = lambda k: pltpu.SemaphoreType.DMA((k,))
     vm = pl.BlockSpec(memory_space=pltpu.VMEM)
-    pairs = [2, nz, 2 * nz, 2 * nz, 4 * nz, 4 * nz, 2 * nz, nz, n]
+    pairs = [2, 2 * nz, 2 * nz, 2 * nz, 4 * nz, 4 * nz, 2 * nz, nz, n]
     return pl.pallas_call(
         functools.partial(kernel, nb),
         out_shape=(
@@ -264,9 +298,12 @@
             jax.ShapeDtypeStruct((r, dout), F32),
             jax.ShapeDtypeStruct((8, 128), F32),
         ),
-        in_specs=[vm] * 3,
+        in_specs=[pl.BlockSpec(memory_space=pl.ANY)] * 2 + [vm],
         out_specs=(vm,) * 3,
         scratch_shapes=[
+            pltpu.VMEM((tok, din), BF16),
+            pltpu.VMEM((tok, dout), BF16),
+            dma(2),
             pltpu.VMEM((tok, din), BF16),
             pltpu.VMEM((tok, dout), BF16),
             pltpu.VMEM((nb * r, tok), BF16),

time: 156 us -> 145 us (0.929)
  Pallas kernels: 146 us -> 135 us
    pallas_call x1, Pallas kernels: 146 us -> 135 us  [fused(): pl.pallas_call(functools.partial(kernel, nb), out_shape=(jax.ShapeDtypeSt...]
where the time goes in v2:
time: 145 us
  Pallas kernels  135 us (93%)
  other arithmetic  6.88 us (5%)
  local copies, waits for them, and re-layouts  1.5 us (1%)
    pallas_call x1, Pallas kernels, fused(): pl.pallas_call(functools.partial(kernel, nb), out_shape=(jax.ShapeDtypeSt...  135 us
    sub x1, other arithmetic, on_device(): master - 0.01 * (first_hat / (jnp.sqrt(second_hat) + 1e-08) + 0.1 * master)  3.65 us

profile of v2, /device:TPU:0, one launch (start us, length us, event | category | flops | bytes accessed | tf_op | source)
XLA Modules:
  0.0 144.5 jit_solution(1295256225076843471)
XLA Ops:
  0.6 1.9 %convert_element_type.3.w_ref = bf16[80,2560]{1,0:T(8,128)(2,1)} convert(f32[80,2560]{1,0:T(8,128)} %param.7) | non-fusion elementwise | flops 204800 | bytes 1228800 | tf_op jit(solution)/shard_map/convert_element_type | solution.py:347
  2.6 0.0 copy-start
  2.6 134.7 %shard_map.84 = (bf16[512,2560]{1,0:T(8,128)(2,1)}, f32[80,2560]{1,0:T(8,128)}, f32[8,128]{1,0:T(8,128)}) custom-call(bf16[512,2560]{1,0:T(8,128)(2,1)} %attn_hbm.1, bf16[512,2560]{1,0:T(8,128)(2,1)} %og_hbm.1, bf16[80,2560]{1,0:T(8,128)(2,1)} %convert_element_type.3.w_ref), custom_call_target="tpu_custom_call" | custom-call | tf_op jit(solution)/shard_map/pallas_call | solution.py:294
  137.3 1.3 reduce_sum.9
  139.3 0.0 copy-done
  139.3 0.0 copy-start.1
  139.4 3.7 %multiply_subtract_fusion = (f32[80,2560]{1,0:T(8,128)}, f32[80,2560]{1,0:T(8,128)}, f32[80,2560]{1,0:T(8,128)}) fusion(f32[80,2560]{1,0:T(8,128)S(1)} %copy-done, f32[80,2560]{1,0:T(8,128)} %get-tuple-element.8, f32[]{:T(128)S(6)} %min_shard_map.3, f32[80,2560]{1,0:T(8,128)} %param.8, f32[80,2560]{1,0:T(8,128)} %param.9), kind=kLoop, calls=%fused_computation.2 | loop fusion | flops 3276800 | bytes 5734404 | tf_op jit(solution)/shard_map/sub | solution.py:362
  143.0 0.0 copy-done.1
  143.0 1.5 %copy.10 = bf16[512,2560]{1,0:T(8,128)(2,1)} copy(bf16[512,2560]{1,0:T(8,128)(2,1)S(1)} %copy-done.1) | data formatting | bytes 5242880
Async XLA Ops:
  2.6 136.8 %copy-start = (f32[80,2560]{1,0:T(8,128)S(1)}, f32[80,2560]{1,0:T(8,128)}, u32[]{:S(2)}) copy-start(f32[80,2560]{1,0:T(8,128)} %param.7) | copy-start | bytes 2457604
  139.3 3.7 %copy-start.1 = (bf16[512,2560]{1,0:T(8,128)(2,1)S(1)}, bf16[512,2560]{1,0:T(8,128)(2,1)}, u32[]{:S(2)}) copy-start(bf16[512,2560]{1,0:T(8,128)(2,1)} %get-tuple-element.17) | copy-start | bytes 7864324
